TPU v7x, 128 devices: a whole 4x4x4 slice. The times are simulated.
128 devices in a mesh: dp: 1, tp: 2 (over core), sp: 64 (over z, y, x).
Axes of the slice: x: 4, y: 4, z: 4, core: 2. Of those that a mesh axis runs over, the one named last changes fastest.
Arguments:
- hidden: bfloat16 [8, 5120], P('dp')
- lengths: int32 [8], P('dp')
- k_cache: bfloat16 [8, 16384, 8, 128], P('dp', 'sp', 'tp')
- v_cache: bfloat16 [8, 16384, 8, 128], P('dp', 'sp', 'tp')
- norm_gain: bfloat16 [5120], replicated
- w_q: bfloat16 [5120, 4096], P(None, 'tp')
- w_k: bfloat16 [5120, 1024], P(None, 'tp')
- w_v: bfloat16 [5120, 1024], P(None, 'tp')
- w_o: bfloat16 [4096, 5120], P('tp')
- inv_freq: float32 [64], replicated
Outputs:
- output 1: bfloat16 [8, 5120], P('dp')
- output 2: bfloat16 [8, 16384, 8, 128], P('dp', 'sp', 'tp')
- output 3: bfloat16 [8, 16384, 8, 128], P('dp', 'sp', 'tp')
All inputs are finite; a program needn't handle non-finite values.
Results may differ from a plain program's by a relative error of at most 0.00639264.
Values sent between devices are 32-bit elements.
A program may use at most 1 GiB of HBM per device.

v0:
```python
import jax
import jax.numpy as jnp
from jax import lax
from jax.sharding import PartitionSpec as P

NORM_EPS = 1e-5
NEG_BIG = -1e30


def rms_norm(hidden, norm_gain):
    hidden_f32 = hidden.astype(jnp.float32)
    inv_rms = lax.rsqrt(jnp.mean(hidden_f32 * hidden_f32, axis=-1, keepdims=True) + NORM_EPS)
    return (hidden_f32 * inv_rms * norm_gain.astype(jnp.float32)).astype(jnp.bfloat16)


def apply_rope(head_vec, angles):
    half_dim = head_vec.shape[-1] // 2
    vec_f32 = head_vec.astype(jnp.float32)
    cos_ang = jnp.cos(angles)[:, None, :]
    sin_ang = jnp.sin(angles)[:, None, :]
    lo_half = vec_f32[..., :half_dim]
    hi_half = vec_f32[..., half_dim:]
    rotated = jnp.concatenate([lo_half * cos_ang - hi_half * sin_ang, hi_half * cos_ang + lo_half * sin_ang], axis=-1)
    return rotated.astype(jnp.bfloat16)


def project_new_token(hidden, lengths, norm_gain, w_q, w_k, w_v, inv_freq):
    batch_size = hidden.shape[0]
    head_dim = 2 * inv_freq.shape[0]
    normed = rms_norm(hidden, norm_gain)
    q_heads = jnp.dot(normed, w_q, preferred_element_type=jnp.float32).astype(jnp.bfloat16).reshape(batch_size, -1, head_dim)
    k_new = jnp.dot(normed, w_k, preferred_element_type=jnp.float32).astype(jnp.bfloat16).reshape(batch_size, -1, head_dim)
    v_new = jnp.dot(normed, w_v, preferred_element_type=jnp.float32).astype(jnp.bfloat16).reshape(batch_size, -1, head_dim)
    angles = lengths.astype(jnp.float32)[:, None] * inv_freq[None, :]
    return apply_rope(q_heads, angles), apply_rope(k_new, angles), v_new


def write_and_attend(q_rot, k_rot, v_new, lengths, k_cache, v_cache):
    batch_size, slot_count, kv_local, head_dim = k_cache.shape
    slot_start = lax.axis_index('sp') * slot_count
    local_pos = lengths - slot_start
    owned = (local_pos >= 0) & (local_pos < slot_count)
    write_pos = jnp.where(owned, local_pos, slot_count)
    row_ids = jnp.arange(batch_size)
    k_upd = k_cache.at[row_ids, write_pos].set(k_rot, mode='drop')
    v_upd = v_cache.at[row_ids, write_pos].set(v_new, mode='drop')
    group_size = q_rot.shape[1] // kv_local
    q_grp = q_rot.reshape(batch_size, kv_local, group_size, head_dim)
    scores = jnp.einsum('bkgd,bskd->bkgs', q_grp, k_upd, preferred_element_type=jnp.float32) * head_dim ** -0.5
    valid_mask = ((slot_start + jnp.arange(slot_count))[None, :] <= lengths[:, None])[:, None, None, :]
    scores = jnp.where(valid_mask, scores, NEG_BIG)
    part_max = jnp.max(scores, axis=-1)
    weights = jnp.where(valid_mask, jnp.exp(scores - part_max[..., None]), 0.0)
    part_sum = jnp.sum(weights, axis=-1)
    part_out = jnp.einsum('bkgs,bskd->bkgd', weights.astype(jnp.bfloat16), v_upd, preferred_element_type=jnp.float32)
    return k_upd, v_upd, part_max, part_sum, part_out


def device_step(hidden, lengths, k_cache, v_cache, norm_gain, w_q, w_k, w_v, w_o, inv_freq):
    batch_size = hidden.shape[0]
    q_rot, k_rot, v_new = project_new_token(hidden, lengths, norm_gain, w_q, w_k, w_v, inv_freq)
    k_upd, v_upd, part_max, part_sum, part_out = write_and_attend(q_rot, k_rot, v_new, lengths, k_cache, v_cache)
    all_max = lax.all_gather(part_max, 'sp')
    all_sum = lax.all_gather(part_sum, 'sp')
    all_out = lax.all_gather(part_out, 'sp')
    top_score = jnp.max(all_max, axis=0)
    factor = jnp.exp(all_max - top_score[None])
    weighted = jnp.sum(factor[..., None] * all_out, axis=0)
    weight_sum = jnp.sum(factor * all_sum, axis=0)
    attn_out = (weighted / weight_sum[..., None]).astype(jnp.bfloat16).reshape(batch_size, -1)
    proj_out = lax.psum(jnp.dot(attn_out, w_o, preferred_element_type=jnp.float32), 'tp')
    y_out = (hidden.astype(jnp.float32) + proj_out).astype(jnp.bfloat16)
    return y_out, k_upd, v_upd


def solution(mesh):
    cache_spec = P('dp', 'sp', 'tp', None)
    in_specs = (P('dp', None), P('dp'), cache_spec, cache_spec, P(None), P(None, 'tp'), P(None, 'tp'), P(None, 'tp'), P('tp', None), P(None))
    out_specs = (P('dp', None), cache_spec, cache_spec)
    return jax.shard_map(device_step, mesh=mesh, in_specs=in_specs, out_specs=out_specs, check_vma=False)
```

profile of v0, /device:TPU:1, one launch (start us, length us, event | category | flops | bytes accessed | tf_op | source)
XLA Modules:
  0.0 437.0 jit_solution(6585374978072705964)
XLA Ops:
  7.2 0.0 copy-start
  7.2 0.0 copy-start.4
  7.2 0.0 copy-start.3
  7.2 0.0 all-gather.5.cloned.1.call-start
  7.2 3.6 copy.48
  10.9 0.0 copy-done.4
  10.9 0.0 copy-done
  10.9 0.2 fusion.15
  11.1 0.1 broadcast_compare_fusion
  11.2 0.0 copy-done.3
  11.2 3.3 fusion.14
  14.5 3.3 fusion.13
  17.8 0.1 fusion.37
  17.9 0.0 copy-start.5
  17.9 0.0 copy-start.2
  17.9 8.6 %fusion.11 = f32[8,16,128]{2,0,1:T(8,128)S(1)} fusion(bf16[5120,2048]{1,0:T(8,128)(2,1)} %param.15, bf16[8,5120]{1,0:T(8,128)(2,1)S(1)} %copy-done, f32[5120]{0:T(1024)S(1)} %convert_element_type.51, f32[8]{0:T(128)S(1)} %add_rsqrt_fusion), kind=kOutput, calls=%fused_computation.11 | convolution fusion | flops 167968768 | bytes 21139488 | tf_op jit(solution)/shard_map/dot_general | solution.py:31
  26.5 0.0 copy-done.5
  26.5 0.1 multiply_cosine_fusion
  26.6 0.1 subtract_convert_fusion
  26.8 0.1 pad_maximum_fusion
  26.8 2.0 scatter_fusion
  28.9 0.0 copy-done.2
  28.9 0.8 scatter_fusion.1
  29.7 0.0 copy-start.1
  29.7 3.1 fusion.38
  32.8 1.1 fusion
  33.9 0.0 all-gather.5.cloned.1.call-update
  34.0 0.0 copy-done.1
  34.0 0.0 all-reduce.2.cloned.1.call-start
  34.0 157.8 %all-gather = f32[512,4,4]{2,1,0:T(4,128)S(1)} all-gather(f32[8,4,4]{2,1,0:T(4,128)S(1)} %get-tuple-element.11), channel_id=2, replica_groups=mesh['dp'=1,'tp'=2,'sp'=64] {'sp'}, dimensions={0}, use_global_device_ids=true | all-gather | bytes 33280 | tf_op jit(solution)/shard_map/all_gather | solution.py:63
  191.9 0.2 reduce_max.19
  192.1 0.2 fusion.19
  192.3 147.5 %all-gather.2 = f32[512,4,4]{2,1,0:T(4,128)S(1)} all-gather(f32[8,4,4]{2,1,0:T(4,128)S(1)} %fusion.19), channel_id=4, replica_groups=mesh['dp'=1,'tp'=2,'sp'=64] {'sp'}, dimensions={0}, use_global_device_ids=true | all-gather | bytes 33280 | tf_op jit(solution)/shard_map/all_gather | solution.py:64
  339.8 0.4 subtract_exponential_fusion
  340.2 0.5 multiply_reduce_fusion.1
  340.7 0.0 all-gather.5.cloned.1.call-done
  340.7 4.4 %multiply_reduce_fusion = f32[8,4,4,128]{3,2,1,0:T(4,128)S(1)} fusion(f32[64,8,4,4,128]{4,3,2,1,0:T(4,128)} %bitcast.32, f32[64,8,4,4]{3,2,1,0:T(4,128)S(1)} %subtract_exponential_fusion), kind=kLoop, calls=%fused_computation.2 | loop fusion | flops 2080768 | bytes 4292608 | tf_op jit(solution)/shard_map/reduce_sum | solution.py:68
  345.2 0.1 divide_convert_fusion
  345.3 9.1 %fusion.39 = f32[8,5120]{1,0:T(8,128)} fusion(bf16[8,2048]{1,0:T(8,128)(2,1)S(1)} %convert_element_type.63, bf16[2048,5120]{1,0:T(8,128)(2,1)} %param.18), kind=kOutput, calls=%fused_computation.59 | convolution fusion | flops 167772160 | bytes 21168128 | tf_op jit(solution)/shard_map/dot_general | solution.py:71
  354.4 0.0 all-reduce.2.cloned.1.call-update
  354.4 74.1 %all-reduce.2.cloned.1.call-done = f32[8,5120]{1,0:T(8,128)} async-done(((f32[8,5120]{1,0:T(8,128)}), f32[8,5120]{1,0:T(8,128)}) %all-reduce.2.cloned.1.call-update) | async-done | bytes 163856 | tf_op jit(solution)/shard_map/psum | solution.py:71
  428.6 1.6 fusion.18
  (10 shorter events, 0.1 us)
Async XLA Ops:
  7.2 3.7 copy-start
  7.2 3.7 copy-start.4
  7.2 4.0 copy-start.3
  7.2 333.5 %all-gather.5.cloned.1.call-start = ((), (), s32[]{:S(2)}) async-start(), calls=%async_computation.1 | async-start | bytes 4259840 | tf_op jit(solution)/shard_map/all_gather | solution.py:65
  17.9 8.6 %copy-start.5 = (f32[64]{0:T(128)S(1)}, f32[64]{0:T(128)}, u32[]{:S(2)}) copy-start(f32[64]{0:T(128)} %param.19) | copy-start | bytes 772
  17.9 11.0 %copy-start.2 = (bf16[8,256,4,128]{3,2,1,0:T(4,128)(2,1)S(1)}, bf16[8,256,4,128]{3,2,1,0:T(4,128)(2,1)}, u32[]{:S(2)}) copy-start(bf16[8,256,4,128]{3,2,1,0:T(4,128)(2,1)} %param.13) | copy-start | bytes 6291460
  29.7 4.2 copy-start.1
  34.0 394.6 %all-reduce.2.cloned.1.call-start = ((), (), s32[]{:S(2)}) async-start(), calls=%async_computation | async-start | bytes 327680 | tf_op jit(solution)/shard_map/psum | solution.py:71
Sparse Core Ops, SparseCore 0:
  34.1 69.8 all-gather.4
  354.6 73.9 all-reduce.1
where the time goes:
time: 438 us; the launch traced here: 437 us
  blocking collectives  305 us (70%)
  waiting for transfers between devices  74.2 us (17%)
  matrix products  28.5 us (7%)
  between operations  14.2 us (3%)
  other arithmetic  8.01 us (2%)
  local copies, waits for them, and re-layouts  6.63 us (2%)
    all_gather x1, blocking collectives, device_step(): all_max = lax.all_gather(part_max, 'sp')  158 us
    all_gather x1, blocking collectives, device_step(): all_sum = lax.all_gather(part_sum, 'sp')  148 us
    psum x1, waiting for transfers between devices, device_step(): lax.psum(jnp.dot(attn_out, w_o, preferred_element_type=jnp.float32), 'tp')  74.1 us
    dot_general x1, matrix products, device_step(): jnp.dot(attn_out, w_o, preferred_element_type=jnp.float32)  9.09 us
  transfers between devices with their start and end apart: 2, of which 1 were waited for; matrix products, arithmetic and copies ran while one was open for 0% of the time, Pallas kernels for 0%

commit v1 on v0

v1 whole, which is shorter than its diff:
```python
import functools

import jax
import jax.numpy as jnp
from jax import lax
from jax.experimental import pallas as pl
from jax.experimental.pallas import tpu as pltpu
from jax.sharding import PartitionSpec as P

MESH = pl.DeviceIdType.MESH
ANY = pl.BlockSpec(memory_space=pltpu.HBM)
VMEM = pl.BlockSpec(memory_space=pltpu.VMEM)
SMEM = pl.BlockSpec(memory_space=pltpu.SMEM)

NORM_EPS = 1e-5
NEG_BIG = -1e30
SIDE = 4
VMEM_LIMIT = 58 << 20
CHUNK = 1024


def coords(me):
    return lax.rem(me, SIDE), lax.rem(me // SIDE, SIDE), me // (SIDE * SIDE)


def torus_offsets():
    hops = lambda t: min(t, SIDE - t)
    all_offs = [(a, b, c) for a in range(SIDE) for b in range(SIDE) for c in range(SIDE) if a + b + c]
    return sorted(all_offs, key=lambda t: -(hops(t[0]) + hops(t[1]) + hops(t[2])))


def rope(vec, cos_full, sin_full):
    return vec * cos_full + pltpu.roll(vec, 64, 1) * sin_full


def bf16_round(val):
    return val.astype(jnp.bfloat16).astype(jnp.float32)


def decode_kernel(x_hbm, len_hbm, gain_hbm, wq_hbm, wk_hbm, wv_hbm, wo_hbm, freq_hbm, kc_hbm, vc_hbm, y_ref, k_ref, v_ref,
                  x_buf, gain_buf, freq_buf, len_buf, normed, wq_buf, wkv_buf, wo_buf, pieces, q_buf, k_new, v_new, new_score,
                  send, recv, heads, total, other,
                  small_sem, wq_sem, wkv_sem, cache_sem, wo_sem, piece_sems, part_sems, head_send_sem, head_sem, tp_sems):
    me = lax.axis_index('sp')
    tp = lax.axis_index('tp')
    x, y, z = coords(me)
    xs = [lax.rem(x + d, SIDE) for d in range(SIDE)]
    ys = [SIDE * lax.rem(y + d, SIDE) for d in range(SIDE)]
    zs = [SIDE * SIDE * lax.rem(z + d, SIDE) for d in range(SIDE)]
    sp_ids = [zs[c] + ys[b] + xs[a] for a, b, c in torus_offsets()]
    px, py, pz = lax.rem(x, 2), lax.rem(y, 2), lax.rem(z, 2)
    cx, cy, cz = x // 2, y // 2, z // 2
    my_member = px + 2 * py + 4 * pz
    my_cube = cx + 2 * cy + 4 * cz
    cube_peers = []
    for mask in range(1, 8):
        step = (mask % 2) * (1 - 2 * px) + (mask // 2 % 2) * SIDE * (1 - 2 * py) + (mask // 4) * SIDE * SIDE * (1 - 2 * pz)
        cube_peers.append(me + step)

    small = [pltpu.make_async_copy(src, dst, small_sem.at[i])
             for i, (src, dst) in enumerate([(x_hbm, x_buf), (gain_hbm, gain_buf), (freq_hbm, freq_buf), (len_hbm, len_buf)])]
    for copy in small:
        copy.start()
    steps = wq_hbm.shape[0] // CHUNK
    q_col = pl.ds(pl.multiple_of(my_member * 256, 256), 256)
    kv_col = pl.ds(pl.multiple_of(lax.rem(my_member, 4) * 128, 128), 128)
    for i in range(steps):
        rows = pl.ds(i * CHUNK, CHUNK)
        pltpu.make_async_copy(wq_hbm.at[rows, q_col], wq_buf.at[rows], wq_sem.at[i]).start()

        @pl.when(my_member < 4)
        def _():
            pltpu.make_async_copy(wk_hbm.at[rows, kv_col], wkv_buf.at[rows], wkv_sem.at[i]).start()

        @pl.when(my_member >= 4)
        def _():
            pltpu.make_async_copy(wv_hbm.at[rows, kv_col], wkv_buf.at[rows], wkv_sem.at[i]).start()

    barrier = pltpu.get_barrier_semaphore()
    for peer in sp_ids:
        pl.semaphore_signal(barrier, inc=1, device_id={'sp': peer}, device_id_type=MESH)
    pl.semaphore_signal(barrier, inc=1, device_id={'tp': 1 - tp}, device_id_type=MESH)

    caches = [pltpu.make_async_copy(kc_hbm, k_ref, cache_sem.at[0]), pltpu.make_async_copy(vc_hbm, v_ref, cache_sem.at[1])]
    for copy in caches:
        copy.start()

    def cube_at(i):
        mask = i + jnp.where(i == 3, 1, 0) - jnp.where(i == 4, 1, 0)
        a, b, c = lax.rem(mask, 2), lax.rem(mask // 2, 2), mask // 4
        return my_cube + a * (1 - 2 * cx) + 2 * b * (1 - 2 * cy) + 4 * c * (1 - 2 * cz)

    def wo_copy(i):
        rows = pl.ds(pl.multiple_of(cube_at(i) * 256, 256), 256)
        return pltpu.make_async_copy(wo_hbm.at[rows], wo_buf.at[i], wo_sem.at[i])

    def start_wo(i, carry):
        wo_copy(i).start()
        return carry

    lax.fori_loop(0, 8, start_wo, 0)

    small[0].wait()
    width = x_buf.shape[1]
    square_sum = jnp.zeros((8, 128), jnp.float32)
    for c in range(width // 128):
        val = x_buf[:, c * 128:(c + 1) * 128].astype(jnp.float32)
        square_sum = square_sum + val * val
    inv_rms = lax.rsqrt(jnp.sum(square_sum, axis=1, keepdims=True) / width + NORM_EPS)
    small[1].wait()
    for c in range(width // 128):
        val = x_buf[:, c * 128:(c + 1) * 128].astype(jnp.float32)
        normed[:, c * 128:(c + 1) * 128] = (val * inv_rms * gain_buf[c:c + 1, :].astype(jnp.float32)).astype(jnp.bfloat16)
    small[2].wait()
    small[3].wait()
    row_ids = lax.broadcasted_iota(jnp.int32, (8, 64), 0)
    pos = jnp.zeros((8, 64), jnp.int32)
    for b in range(8):
        pos = jnp.where(row_ids == b, len_buf[b], pos)
    angles = pos.astype(jnp.float32) * freq_buf[...]
    cos_ang, sin_ang = jnp.cos(angles), jnp.sin(angles)
    cos_full = jnp.concatenate([cos_ang, cos_ang], axis=1)
    sin_full = jnp.concatenate([-sin_ang, sin_ang], axis=1)
    acc_q = jnp.zeros((8, 256), jnp.float32)
    acc_kv = jnp.zeros((8, 128), jnp.float32)
    for i in range(steps):
        rows = pl.ds(i * CHUNK, CHUNK)
        lhs = normed[:, i * CHUNK:(i + 1) * CHUNK]
        pltpu.make_async_copy(wq_hbm.at[rows, q_col], wq_buf.at[rows], wq_sem.at[i]).wait()
        acc_q = acc_q + jnp.dot(lhs, wq_buf[i * CHUNK:(i + 1) * CHUNK, :], preferred_element_type=jnp.float32)
        pltpu.make_async_copy(wk_hbm.at[rows, kv_col], wkv_buf.at[rows], wkv_sem.at[i]).wait()
        acc_kv = acc_kv + jnp.dot(lhs, wkv_buf[i * CHUNK:(i + 1) * CHUNK, :], preferred_element_type=jnp.float32)
    acc_q, acc_kv = bf16_round(acc_q), bf16_round(acc_kv)
    pieces[my_member, 0] = bf16_round(rope(acc_q[:, :128], cos_full, sin_full))
    pieces[my_member, 1] = bf16_round(rope(acc_q[:, 128:], cos_full, sin_full))
    pieces[my_member, 2] = jnp.where(my_member < 4, bf16_round(rope(acc_kv, cos_full, sin_full)), acc_kv)

    pl.semaphore_wait(barrier, len(sp_ids) + 1)
    for peer in cube_peers:
        pltpu.make_async_remote_copy(pieces.at[my_member], pieces.at[my_member], piece_sems.at[0], piece_sems.at[1],
                                     device_id={'sp': peer}, device_id_type=MESH).start()
    seven = pieces.at[pl.ds(0, 7)]
    pltpu.make_async_copy(seven, seven, piece_sems.at[1]).wait()
    for j in range(8):
        q_buf[j * 16:j * 16 + 8, :] = pieces[j, 0]
        q_buf[j * 16 + 8:j * 16 + 16, :] = pieces[j, 1]
    for h in range(16):
        new_score[h * 8:h * 8 + 8, :] = jnp.broadcast_to(
            jnp.sum(q_buf[h * 8:h * 8 + 8, :] * pieces[h // 4, 2], axis=1, keepdims=True) * 128 ** -0.5, (8, 128))
        v_new[h * 8:h * 8 + 8, :] = pieces[4 + h // 4, 2]
    for j in range(4):
        k_new[j * 8:j * 8 + 8, :] = pieces[j, 2]

    for copy in caches:
        copy.wait()
    slots = k_ref.shape[0] // 32
    lanes = lax.broadcasted_iota(jnp.int32, (16, slots * 4), 1)
    head_ids = lax.broadcasted_iota(jnp.int32, (16, slots * 4), 0)
    same_head = lax.rem(lanes, 4) == head_ids // 4
    slot_ids = me * slots + lanes // 4

    def one_batch(b, carry):
        rows = pl.ds(pl.multiple_of(b * slots * 4, slots * 4), slots * 4)
        every = pl.ds(b, 16, stride=8)
        q = q_buf[every, :].astype(jnp.bfloat16)
        scores = lax.dot_general(q, k_ref[rows, :], (((1,), (1,)), ((), ())), preferred_element_type=jnp.float32) * 128 ** -0.5
        valid = same_head & (slot_ids < len_buf[b])
        local = jnp.zeros((16, 1), jnp.int32) + (len_buf[b] - me * slots)
        owned = (local >= 0) & (local < slots)
        last = jnp.where(owned, new_score[every, :][:, :1], NEG_BIG)
        scores = jnp.where(valid, scores, NEG_BIG)
        top = jnp.maximum(jnp.max(scores, axis=1, keepdims=True), last)
        weights = jnp.where(valid, jnp.exp(scores - top), 0.0)
        last_weight = jnp.where(owned, jnp.exp(last - top), 0.0)
        weight_sum = jnp.sum(weights, axis=1, keepdims=True) + last_weight
        out = jnp.dot(weights.astype(jnp.bfloat16), v_ref[rows, :], preferred_element_type=jnp.float32)
        out = out + bf16_round(last_weight) * v_new[every, :]
        some = weight_sum > 0.0
        safe = jnp.where(some, weight_sum, 1.0)
        out = jnp.where(some, out / safe, 0.0)
        log_sum = jnp.broadcast_to(jnp.where(some, top + jnp.log(safe), NEG_BIG), (16, 128))
        for pair in range(8):
            send[b * 8 + pair, 0:2, :] = out[2 * pair:2 * pair + 2]
            send[b * 8 + pair, 2:4, :] = log_sum[2 * pair:2 * pair + 2]
        return carry

    lax.fori_loop(0, 8, one_batch, 0)

    def cube_of(peer):
        u, v, w = coords(peer)
        return u // 2 + 2 * (v // 2) + 4 * (w // 2)

    def member_of(peer):
        u, v, w = coords(peer)
        return lax.rem(u, 2) + 2 * lax.rem(v, 2) + 4 * lax.rem(w, 2)

    for peer in sp_ids:
        pltpu.make_async_remote_copy(send.at[member_of(peer) * 8 + cube_of(peer)], recv.at[me], part_sems.at[0], part_sems.at[1],
                                     device_id={'sp': peer}, device_id_type=MESH).start()
    recv[me] = send[my_member * 8 + my_cube]

    tile_slots = lax.broadcasted_iota(jnp.int32, (16, 128), 0) // 4

    def update(b, carry):
        local = len_buf[b] - me * slots
        news = [jnp.concatenate([new] * 4, axis=0).astype(jnp.bfloat16)
                for new in (k_new[pl.ds(b, 4, stride=8), :], v_new[pl.ds(b, 4, stride=32), :])]

        def put(i, carry):
            for j in range(8):
                at = pl.ds(pl.multiple_of((b * (slots // 4) + i * 8 + j) * 16, 16), 16)
                hit = tile_slots + (i * 8 + j) * 4 == local
                k_ref[at, :] = jnp.where(hit, news[0], k_ref[at, :])
                v_ref[at, :] = jnp.where(hit, news[1], v_ref[at, :])
            return carry

        lax.fori_loop(0, slots // 32, put, 0)
        return carry

    lax.fori_loop(0, 8, update, 0)

    most = recv.at[pl.ds(0, 63)]
    pltpu.make_async_copy(most, most, part_sems.at[1]).wait()
    best = recv[0, 2:4, :]
    for i in range(1, 64):
        best = jnp.maximum(best, recv[i, 2:4, :])
    weighted = jnp.zeros((2, 128), jnp.float32)
    factor_sum = jnp.zeros((2, 128), jnp.float32)
    for i in range(64):
        factor = jnp.exp(recv[i, 2:4, :] - best)
        weighted = weighted + factor * recv[i, 0:2, :]
        factor_sum = factor_sum + factor
    heads[my_cube, my_member] = bf16_round(weighted / factor_sum)

    for peer in sp_ids:
        pltpu.make_async_remote_copy(heads.at[my_cube, my_member], heads.at[my_cube, my_member], head_send_sem, head_sem.at[my_cube],
                                     device_id={'sp': peer}, device_id_type=MESH).start()
    total[...] = jnp.zeros_like(total)

    def one_block(i, carry):
        cube = cube_at(i)

        @pl.when(i == 0)
        def _():
            members = heads.at[cube, pl.ds(0, 7)]
            pltpu.make_async_copy(members, members, head_sem.at[cube]).wait()

        @pl.when(i > 0)
        def _():
            pltpu.make_async_copy(heads.at[cube], heads.at[cube], head_sem.at[cube]).wait()

        wo_copy(i).wait()
        lhs = jnp.concatenate([heads[cube, :, 0, :], heads[cube, :, 1, :]], axis=1).astype(jnp.bfloat16)
        total[...] += jnp.dot(lhs, wo_buf[i], preferred_element_type=jnp.float32)
        return carry

    lax.fori_loop(0, 8, one_block, 0)

    swap = pltpu.make_async_remote_copy(total, other, tp_sems.at[0], tp_sems.at[1], device_id={'tp': 1 - tp}, device_id_type=MESH)
    swap.start()
    pltpu.make_async_copy(seven, seven, piece_sems.at[0]).wait()
    pltpu.make_async_copy(most, most, part_sems.at[0]).wait()
    sent = heads.at[pl.ds(0, 7)]
    pltpu.make_async_copy(sent, sent, head_send_sem).wait()
    sent = heads.at[0, pl.ds(0, 7)]
    pltpu.make_async_copy(sent, sent, head_send_sem).wait()
    swap.wait()
    y_ref[...] = (x_buf[...].astype(jnp.float32) + (total[...] + other[...])).astype(jnp.bfloat16)


def device_step(hidden, lengths, k_cache, v_cache, norm_gain, w_q, w_k, w_v, w_o, inv_freq):
    batch, width = hidden.shape
    f32, bf16 = jnp.float32, jnp.bfloat16
    dma = pltpu.SemaphoreType.DMA
    steps = width // CHUNK
    rows = k_cache.shape[0] * k_cache.shape[1] * k_cache.shape[2]
    flat = jax.ShapeDtypeStruct((rows, 128), bf16)
    y_out, k_upd, v_upd = pl.pallas_call(
        decode_kernel,
        out_shape=[jax.ShapeDtypeStruct((batch, width), bf16), flat, flat],
        in_specs=[ANY] * 10,
        out_specs=[VMEM] * 3,
        scratch_shapes=[
            pltpu.VMEM((batch, width), bf16), pltpu.VMEM((width // 128, 128), bf16), pltpu.VMEM((1, 64), f32), pltpu.SMEM((batch,), jnp.int32),
            pltpu.VMEM((batch, width), bf16), pltpu.VMEM((width, 256), bf16), pltpu.VMEM((width, 128), bf16), pltpu.VMEM((8, 256, width), bf16),
            pltpu.VMEM((8, 3, 8, 128), f32), pltpu.VMEM((128, 128), f32), pltpu.VMEM((32, 128), f32), pltpu.VMEM((128, 128), f32),
            pltpu.VMEM((128, 128), f32), pltpu.VMEM((64, 4, 128), f32), pltpu.VMEM((64, 4, 128), f32), pltpu.VMEM((8, 8, 2, 128), f32),
            pltpu.VMEM((batch, width), f32), pltpu.VMEM((batch, width), f32),
            dma((4,)), dma((steps,)), dma((steps,)), dma((2,)), dma((8,)), dma((2,)), dma((2,)), dma, dma((8,)), dma((2,)),
        ],
        compiler_params=pltpu.CompilerParams(collective_id=0, has_side_effects=True, vmem_limit_bytes=VMEM_LIMIT),
        name='decode',
    )(hidden, lengths, norm_gain.reshape(width // 128, 128), w_q, w_k, w_v, w_o, inv_freq.reshape(1, 64),
      k_cache.reshape(rows, 128), v_cache.reshape(rows, 128))
    return y_out, k_upd.reshape(k_cache.shape), v_upd.reshape(v_cache.shape)


def solution(mesh):
    cache_spec = P('dp', 'sp', 'tp', None)
    in_specs = (P('dp', None), P('dp'), cache_spec, cache_spec, P(None), P(None, 'tp'), P(None, 'tp'), P(None, 'tp'), P('tp', None), P(None))
    out_specs = (P('dp', None), cache_spec, cache_spec)
    return jax.shard_map(device_step, mesh=mesh, in_specs=in_specs, out_specs=out_specs, check_vma=False)
```

time: 438 us -> 42.6 us (0.10)
  blocking collectives: 305 us -> 0 us
  waiting for transfers between devices: 74.2 us -> 0 us
  Pallas kernels: 0 us -> 35.1 us
  matrix products: 28.5 us -> 0 us
  between operations: 14.2 us -> 0.64 us
  other arithmetic: 8.01 us -> 0 us
    all_gather x2 -> x0, blocking collectives: 305 us -> none  [the longest x1 158 us: device_step(): all_max = lax.all_gather(part_max, 'sp')]
    psum x1 -> x0, waiting for transfers between devices: 74.1 us -> none  [device_step(): lax.psum(jnp.dot(attn_out, w_o, preferred_element_type=jnp.float32), 'tp')]
    pallas_call x0 -> x1, Pallas kernels: none -> 35.1 us  [device_step(): pl.pallas_call(decode_kernel, out_shape=[jax.ShapeDtypeStruct((batch, wid...]
    dot_general x6 -> x0, matrix products: 28.5 us -> none  [the longest x1 9.09 us: device_step(): jnp.dot(attn_out, w_o, preferred_element_type=jnp.float32)]
    reduce_sum x4 -> x0, other arithmetic: 5.32 us -> none  [the longest x1 4.44 us: device_step(): weighted = jnp.sum(factor[..., None] * all_out, axis=0)]
  transfers between devices with their start and end apart: 2 -> 0, of which waited for: 1 -> 0; matrix products, arithmetic and copies ran while one was open for 0% -> 0% of each run, Pallas kernels for 0% -> 0%
where the time goes in v1:
time: 42.6 us; the launch traced here: 42.4 us
  Pallas kernels  35.1 us (82%)
  local copies, waits for them, and re-layouts  6.63 us (16%)
  between operations  0.64 us (2%)
    pallas_call x1, Pallas kernels, device_step(): pl.pallas_call(decode_kernel, out_shape=[jax.ShapeDtypeStruct((batch, wid...  35.1 us
    unnamed x5, local copies, waits for them, and re-layouts  6.63 us

profile of v1, /device:TPU:1, one launch (start us, length us, event | category | flops | bytes accessed | tf_op | source)
XLA Modules:
  0.0 42.4 jit_solution(1686388698581552147)
XLA Ops:
  0.6 35.1 %decode.1 = (bf16[8,5120]{1,0:T(8,128)(2,1)}, bf16[8192,128]{1,0:T(8,128)(2,1)}, bf16[8192,128]{1,0:T(8,128)(2,1)}) custom-call(bf16[8,5120]{1,0:T(8,128)(2,1)} %x_hbm.1, s32[8]{0:T(128)} %len_hbm.1, bf16[40,128]{1,0:T(8,128)(2,1)} %bitcast.10, bf16[5120,2048]{1,0:T(8,128)(2,1)} %wq_hbm.1, bf16[5120,512]{1,0:T(8,128)(2,1)} %wk_hbm.1, ...), custom_call_target="tpu_custom_call" | custom-call | tf_op jit(solution)/shard_map/decode/pallas_call | solution.py:278
  35.8 1.5 %copy.16 = bf16[8,5120]{1,0:T(8,128)(2,1)} copy(bf16[8,5120]{1,0:T(8,128)(2,1)} %get-tuple-element.12) | data formatting | bytes 163840
  37.3 0.0 copy-start
  37.3 3.8 %copy.17 = bf16[8,256,4,128]{3,2,1,0:T(4,128)(2,1)} copy(bf16[8,256,4,128]{3,2,1,0:T(4,128)(2,1)} %bitcast.9) | data formatting | bytes 4194304
  41.1 0.0 copy-done
  41.1 1.3 %copy.18 = bf16[8,256,4,128]{3,2,1,0:T(4,128)(2,1)} copy(bf16[8,256,4,128]{3,2,1,0:T(4,128)(2,1)S(1)} %bitcast.8) | data formatting | bytes 4194304
Async XLA Ops:
  37.3 3.8 %copy-start = (bf16[8192,128]{1,0:T(8,128)(2,1)S(1)}, bf16[8192,128]{1,0:T(8,128)(2,1)}, u32[]{:S(2)}) copy-start(bf16[8192,128]{1,0:T(8,128)(2,1)} %get-tuple-element.8) | copy-start | bytes 6291460

commit v2 on v1

--- a/solution.py
+++ b/solution.py
@@ -15,7 +15,8 @@
 NORM_EPS = 1e-5
 NEG_BIG = -1e30
 SIDE = 4
-VMEM_LIMIT = 58 << 20
+VMEM_LIMIT = 59 << 20
+GROUP = 4
 CHUNK = 1024
 
 
@@ -39,7 +40,7 @@
 
 def decode_kernel(x_hbm, len_hbm, gain_hbm, wq_hbm, wk_hbm, wv_hbm, wo_hbm, freq_hbm, kc_hbm, vc_hbm, y_ref, k_ref, v_ref,
                   x_buf, gain_buf, freq_buf, len_buf, normed, wq_buf, wkv_buf, wo_buf, pieces, q_buf, k_new, v_new, new_score,
-                  send, recv, heads, total, other,
+                  send_lo, send_hi, recv, heads, total, other,
                   small_sem, wq_sem, wkv_sem, cache_sem, wo_sem, piece_sems, part_sems, head_send_sem, head_sem, tp_sems):
     me = lax.axis_index('sp')
     tp = lax.axis_index('tp')
@@ -59,8 +60,8 @@
 
     small = [pltpu.make_async_copy(src, dst, small_sem.at[i])
              for i, (src, dst) in enumerate([(x_hbm, x_buf), (gain_hbm, gain_buf), (freq_hbm, freq_buf), (len_hbm, len_buf)])]
-    for copy in small:
-        copy.start()
+    for i in (3, 2, 0, 1):
+        small[i].start()
     steps = wq_hbm.shape[0] // CHUNK
     q_col = pl.ds(pl.multiple_of(my_member * 256, 256), 256)
     kv_col = pl.ds(pl.multiple_of(lax.rem(my_member, 4) * 128, 128), 128)
@@ -81,10 +82,6 @@
         pl.semaphore_signal(barrier, inc=1, device_id={'sp': peer}, device_id_type=MESH)
     pl.semaphore_signal(barrier, inc=1, device_id={'tp': 1 - tp}, device_id_type=MESH)
 
-    caches = [pltpu.make_async_copy(kc_hbm, k_ref, cache_sem.at[0]), pltpu.make_async_copy(vc_hbm, v_ref, cache_sem.at[1])]
-    for copy in caches:
-        copy.start()
-
     def cube_at(i):
         mask = i + jnp.where(i == 3, 1, 0) - jnp.where(i == 4, 1, 0)
         a, b, c = lax.rem(mask, 2), lax.rem(mask // 2, 2), mask // 4
@@ -98,8 +95,16 @@
         wo_copy(i).start()
         return carry
 
-    lax.fori_loop(0, 8, start_wo, 0)
-
+    small[2].wait()
+    small[3].wait()
+    row_ids = lax.broadcasted_iota(jnp.int32, (8, 64), 0)
+    pos = jnp.zeros((8, 64), jnp.int32)
+    for b in range(8):
+        pos = jnp.where(row_ids == b, len_buf[b], pos)
+    angles = pos.astype(jnp.float32) * freq_buf[...]
+    cos_ang, sin_ang = jnp.cos(angles), jnp.sin(angles)
+    cos_full = jnp.concatenate([cos_ang, cos_ang], axis=1)
+    sin_full = jnp.concatenate([-sin_ang, sin_ang], axis=1)
     small[0].wait()
     width = x_buf.shape[1]
     square_sum = jnp.zeros((8, 128), jnp.float32)
@@ -111,16 +116,6 @@
     for c in range(width // 128):
         val = x_buf[:, c * 128:(c + 1) * 128].astype(jnp.float32)
         normed[:, c * 128:(c + 1) * 128] = (val * inv_rms * gain_buf[c:c + 1, :].astype(jnp.float32)).astype(jnp.bfloat16)
-    small[2].wait()
-    small[3].wait()
-    row_ids = lax.broadcasted_iota(jnp.int32, (8, 64), 0)
-    pos = jnp.zeros((8, 64), jnp.int32)
-    for b in range(8):
-        pos = jnp.where(row_ids == b, len_buf[b], pos)
-    angles = pos.astype(jnp.float32) * freq_buf[...]
-    cos_ang, sin_ang = jnp.cos(angles), jnp.sin(angles)
-    cos_full = jnp.concatenate([cos_ang, cos_ang], axis=1)
-    sin_full = jnp.concatenate([-sin_ang, sin_ang], axis=1)
     acc_q = jnp.zeros((8, 256), jnp.float32)
     acc_kv = jnp.zeros((8, 128), jnp.float32)
     for i in range(steps):
@@ -130,6 +125,9 @@
         acc_q = acc_q + jnp.dot(lhs, wq_buf[i * CHUNK:(i + 1) * CHUNK, :], preferred_element_type=jnp.float32)
         pltpu.make_async_copy(wk_hbm.at[rows, kv_col], wkv_buf.at[rows], wkv_sem.at[i]).wait()
         acc_kv = acc_kv + jnp.dot(lhs, wkv_buf[i * CHUNK:(i + 1) * CHUNK, :], preferred_element_type=jnp.float32)
+    caches = [pltpu.make_async_copy(kc_hbm, k_ref, cache_sem.at[0]), pltpu.make_async_copy(vc_hbm, v_ref, cache_sem.at[1])]
+    for copy in caches:
+        copy.start()
     acc_q, acc_kv = bf16_round(acc_q), bf16_round(acc_kv)
     pieces[my_member, 0] = bf16_round(rope(acc_q[:, :128], cos_full, sin_full))
     pieces[my_member, 1] = bf16_round(rope(acc_q[:, 128:], cos_full, sin_full))
@@ -139,6 +137,7 @@
     for peer in cube_peers:
         pltpu.make_async_remote_copy(pieces.at[my_member], pieces.at[my_member], piece_sems.at[0], piece_sems.at[1],
                                      device_id={'sp': peer}, device_id_type=MESH).start()
+    lax.fori_loop(0, 8, start_wo, 0)
     seven = pieces.at[pl.ds(0, 7)]
     pltpu.make_async_copy(seven, seven, piece_sems.at[1]).wait()
     for j in range(8):
@@ -159,57 +158,74 @@
     same_head = lax.rem(lanes, 4) == head_ids // 4
     slot_ids = me * slots + lanes // 4
 
-    def one_batch(b, carry):
-        rows = pl.ds(pl.multiple_of(b * slots * 4, slots * 4), slots * 4)
-        every = pl.ds(b, 16, stride=8)
-        q = q_buf[every, :].astype(jnp.bfloat16)
-        scores = lax.dot_general(q, k_ref[rows, :], (((1,), (1,)), ((), ())), preferred_element_type=jnp.float32) * 128 ** -0.5
-        valid = same_head & (slot_ids < len_buf[b])
-        local = jnp.zeros((16, 1), jnp.int32) + (len_buf[b] - me * slots)
-        owned = (local >= 0) & (local < slots)
-        last = jnp.where(owned, new_score[every, :][:, :1], NEG_BIG)
-        scores = jnp.where(valid, scores, NEG_BIG)
-        top = jnp.maximum(jnp.max(scores, axis=1, keepdims=True), last)
-        weights = jnp.where(valid, jnp.exp(scores - top), 0.0)
-        last_weight = jnp.where(owned, jnp.exp(last - top), 0.0)
-        weight_sum = jnp.sum(weights, axis=1, keepdims=True) + last_weight
-        out = jnp.dot(weights.astype(jnp.bfloat16), v_ref[rows, :], preferred_element_type=jnp.float32)
-        out = out + bf16_round(last_weight) * v_new[every, :]
-        some = weight_sum > 0.0
-        safe = jnp.where(some, weight_sum, 1.0)
-        out = jnp.where(some, out / safe, 0.0)
-        log_sum = jnp.broadcast_to(jnp.where(some, top + jnp.log(safe), NEG_BIG), (16, 128))
-        for pair in range(8):
-            send[b * 8 + pair, 0:2, :] = out[2 * pair:2 * pair + 2]
-            send[b * 8 + pair, 2:4, :] = log_sum[2 * pair:2 * pair + 2]
-        return carry
-
-    lax.fori_loop(0, 8, one_batch, 0)
-
-    def cube_of(peer):
-        u, v, w = coords(peer)
-        return u // 2 + 2 * (v // 2) + 4 * (w // 2)
-
-    def member_of(peer):
-        u, v, w = coords(peer)
-        return lax.rem(u, 2) + 2 * lax.rem(v, 2) + 4 * lax.rem(w, 2)
-
-    for peer in sp_ids:
-        pltpu.make_async_remote_copy(send.at[member_of(peer) * 8 + cube_of(peer)], recv.at[me], part_sems.at[0], part_sems.at[1],
+    cube_base = [2 * ((cx + a * (1 - 2 * cx)) + SIDE * (cy + b * (1 - 2 * cy)) + SIDE * SIDE * (cz + c * (1 - 2 * cz)))
+                 for c in range(2) for b in range(2) for a in range(2)]
+    cube_id = [my_cube + a * (1 - 2 * cx) + 2 * b * (1 - 2 * cy) + 4 * c * (1 - 2 * cz)
+               for c in range(2) for b in range(2) for a in range(2)]
+
+    def send_part(b, near):
+        peer = cube_base[near] + (b % 2 + b // 2 % 2 * SIDE + b // 4 * SIDE * SIDE)
+        send = send_lo if b < GROUP else send_hi
+        pltpu.make_async_remote_copy(send.at[b % GROUP * 8 + cube_id[near]], recv.at[me], part_sems.at[0], part_sems.at[1],
                                      device_id={'sp': peer}, device_id_type=MESH).start()
-    recv[me] = send[my_member * 8 + my_cube]
-
-    tile_slots = lax.broadcasted_iota(jnp.int32, (16, 128), 0) // 4
+
+    for first in range(0, 8, GROUP):
+        group = range(first, first + GROUP)
+        send = send_lo if first < GROUP else send_hi
+        scores, valid, owned, last = {}, {}, {}, {}
+        for b in group:
+            q = q_buf[pl.ds(b, 16, stride=8), :].astype(jnp.bfloat16)
+            scores[b] = lax.dot_general(q, k_ref[b * slots * 4:(b + 1) * slots * 4, :], (((1,), (1,)), ((), ())),
+                                        preferred_element_type=jnp.float32) * 128 ** -0.5
+        for b in group:
+            valid[b] = same_head & (slot_ids < len_buf[b])
+            local = jnp.zeros((16, 1), jnp.int32) + (len_buf[b] - me * slots)
+            owned[b] = (local >= 0) & (local < slots)
+            last[b] = jnp.where(owned[b], new_score[pl.ds(b, 16, stride=8), :][:, :1], NEG_BIG)
+            scores[b] = jnp.where(valid[b], scores[b], NEG_BIG)
+        for b in group:
+            top = jnp.maximum(jnp.max(scores[b], axis=1, keepdims=True), last[b])
+            weights = jnp.where(valid[b], jnp.exp(scores[b] - top), 0.0)
+            last_weight = jnp.where(owned[b], jnp.exp(last[b] - top), 0.0)
+            weight_sum = jnp.sum(weights, axis=1, keepdims=True) + last_weight
+            out = jnp.dot(weights.astype(jnp.bfloat16), v_ref[b * slots * 4:(b + 1) * slots * 4, :], preferred_element_type=jnp.float32)
+            out = out + bf16_round(last_weight) * v_new[pl.ds(b, 16, stride=8), :]
+            some = weight_sum > 0.0
+            safe = jnp.where(some, weight_sum, 1.0)
+            out = jnp.where(some, out / safe, 0.0)
+            log_sum = jnp.broadcast_to(jnp.where(some, top + jnp.log(safe), NEG_BIG), (16, 128))
+            for pair in range(8):
+                send[b % GROUP * 8 + pair, 0:2, :] = out[2 * pair:2 * pair + 2]
+                send[b % GROUP * 8 + pair, 2:4, :] = log_sum[2 * pair:2 * pair + 2]
+        for near in range(7, 0, -1):
+            for b in group:
+                send_part(b, near)
+        for b in group:
+            @pl.when(my_member != b)
+            def _():
+                send_part(b, 0)
+
+    @pl.when(my_member < GROUP)
+    def _():
+        recv[me] = send_lo[my_member * 8 + my_cube]
+
+    @pl.when(my_member >= GROUP)
+    def _():
+        recv[me] = send_hi[(my_member - GROUP) * 8 + my_cube]
+
+    tile_slots = (lax.broadcasted_iota(jnp.int32, (16, 128), 0) // 4).astype(jnp.bfloat16)
 
     def update(b, carry):
         local = len_buf[b] - me * slots
+        local = jnp.clip(local, -SIDE, slots).astype(jnp.float32)
         news = [jnp.concatenate([new] * 4, axis=0).astype(jnp.bfloat16)
                 for new in (k_new[pl.ds(b, 4, stride=8), :], v_new[pl.ds(b, 4, stride=32), :])]
 
         def put(i, carry):
             for j in range(8):
                 at = pl.ds(pl.multiple_of((b * (slots // 4) + i * 8 + j) * 16, 16), 16)
-                hit = tile_slots + (i * 8 + j) * 4 == local
+                here = jnp.broadcast_to(local - ((i * 8 + j) * 4).astype(jnp.float32), (16, 128)).astype(jnp.bfloat16)
+                hit = tile_slots == here
                 k_ref[at, :] = jnp.where(hit, news[0], k_ref[at, :])
                 v_ref[at, :] = jnp.where(hit, news[1], v_ref[at, :])
             return carry
@@ -268,6 +284,14 @@
     y_ref[...] = (x_buf[...].astype(jnp.float32) + (total[...] + other[...])).astype(jnp.bfloat16)
 
 
+def finish_kernel(y_in, k_in, v_in, y_hbm, k_hbm, v_hbm, sems):
+    copies = [pltpu.make_async_copy(src, dst, sems.at[i]) for i, (src, dst) in enumerate([(k_in, k_hbm), (v_in, v_hbm), (y_in, y_hbm)])]
+    for copy in copies:
+        copy.start()
+    for copy in copies:
+        copy.wait()
+
+
 def device_step(hidden, lengths, k_cache, v_cache, norm_gain, w_q, w_k, w_v, w_o, inv_freq):
     batch, width = hidden.shape
     f32, bf16 = jnp.float32, jnp.bfloat16
@@ -275,16 +299,17 @@
     steps = width // CHUNK
     rows = k_cache.shape[0] * k_cache.shape[1] * k_cache.shape[2]
     flat = jax.ShapeDtypeStruct((rows, 128), bf16)
-    y_out, k_upd, v_upd = pl.pallas_call(
+    small = jax.ShapeDtypeStruct((batch, width), bf16)
+    outs = pl.pallas_call(
         decode_kernel,
-        out_shape=[jax.ShapeDtypeStruct((batch, width), bf16), flat, flat],
+        out_shape=[pltpu.VMEM((batch, width), bf16), pltpu.VMEM((rows, 128), bf16), pltpu.VMEM((rows, 128), bf16)],
         in_specs=[ANY] * 10,
         out_specs=[VMEM] * 3,
         scratch_shapes=[
             pltpu.VMEM((batch, width), bf16), pltpu.VMEM((width // 128, 128), bf16), pltpu.VMEM((1, 64), f32), pltpu.SMEM((batch,), jnp.int32),
             pltpu.VMEM((batch, width), bf16), pltpu.VMEM((width, 256), bf16), pltpu.VMEM((width, 128), bf16), pltpu.VMEM((8, 256, width), bf16),
             pltpu.VMEM((8, 3, 8, 128), f32), pltpu.VMEM((128, 128), f32), pltpu.VMEM((32, 128), f32), pltpu.VMEM((128, 128), f32),
-            pltpu.VMEM((128, 128), f32), pltpu.VMEM((64, 4, 128), f32), pltpu.VMEM((64, 4, 128), f32), pltpu.VMEM((8, 8, 2, 128), f32),
+            pltpu.VMEM((128, 128), f32), pltpu.VMEM((32, 4, 128), f32), pltpu.VMEM((32, 4, 128), f32), pltpu.VMEM((64, 4, 128), f32), pltpu.VMEM((8, 8, 2, 128), f32),
             pltpu.VMEM((batch, width), f32), pltpu.VMEM((batch, width), f32),
             dma((4,)), dma((steps,)), dma((steps,)), dma((2,)), dma((8,)), dma((2,)), dma((2,)), dma, dma((8,)), dma((2,)),
         ],
@@ -292,6 +317,15 @@
         name='decode',
     )(hidden, lengths, norm_gain.reshape(width // 128, 128), w_q, w_k, w_v, w_o, inv_freq.reshape(1, 64),
       k_cache.reshape(rows, 128), v_cache.reshape(rows, 128))
+    y_out, k_upd, v_upd = pl.pallas_call(
+        finish_kernel,
+        out_shape=[small, flat, flat],
+        in_specs=[VMEM] * 3,
+        out_specs=[ANY] * 3,
+        scratch_shapes=[dma((3,))],
+        compiler_params=pltpu.CompilerParams(vmem_limit_bytes=1 << 20),
+        name='finish',
+    )(*outs)
     return y_out, k_upd.reshape(k_cache.shape), v_upd.reshape(v_cache.shape)
 
 

time: 42.6 us -> 33.5 us (0.79)
  local copies, waits for them, and re-layouts: 6.63 us -> 0 us
  Pallas kernels: 35.1 us -> 32.7 us
    unnamed x5 -> x0, local copies, waits for them, and re-layouts: 6.63 us -> none
    pallas_call x1 -> x2, Pallas kernels: 35.1 us -> 32.7 us  [the longest x1 30.7 us: device_step(): pl.pallas_call(decode_kernel, out_shape=[pltpu.VMEM((batch, width), bf16)...]
where the time goes in v2:
time: 33.5 us; the launch traced here: 33.4 us
  Pallas kernels  32.7 us (98%)
  between operations  0.64 us (2%)
    pallas_call x1, Pallas kernels, device_step(): pl.pallas_call(decode_kernel, out_shape=[pltpu.VMEM((batch, width), bf16)...  30.7 us
    pallas_call x1, Pallas kernels, device_step(): pl.pallas_call(finish_kernel, out_shape=[small, flat, flat], in_specs=[VM...  2.04 us

profile of v2, /device:TPU:1, one launch (start us, length us, event | category | flops | bytes accessed | tf_op | source)
XLA Modules:
  0.0 33.4 jit_solution(2812068397913546342)
XLA Ops:
  0.6 30.7 %decode.1 = (bf16[8,5120]{1,0:T(8,128)(2,1)S(1)}, bf16[8192,128]{1,0:T(8,128)(2,1)S(1)}, bf16[8192,128]{1,0:T(8,128)(2,1)S(1)}) custom-call(bf16[8,5120]{1,0:T(8,128)(2,1)} %x_hbm.1, s32[8]{0:T(128)} %len_hbm.1, bf16[40,128]{1,0:T(8,128)(2,1)} %bitcast.8, bf16[5120,2048]{1,0:T(8,128)(2,1)} %wq_hbm.1, bf16[5120,512]{1,0:T(8,128)(2,1)} %wk_hbm.1, ...), custom_call_target="tpu_custom_call" | custom-call | tf_op jit(solution)/shard_map/decode/pallas_call | solution.py:303
  31.3 2.0 %finish.1 = (bf16[8,5120]{1,0:T(8,128)(2,1)}, bf16[8192,128]{1,0:T(8,128)(2,1)}, bf16[8192,128]{1,0:T(8,128)(2,1)}) custom-call(bf16[8,5120]{1,0:T(8,128)(2,1)S(1)} %get-tuple-element.9.y_in, bf16[8192,128]{1,0:T(8,128)(2,1)S(1)} %get-tuple-element.10.k_in, bf16[8192,128]{1,0:T(8,128)(2,1)S(1)} %get-tuple-element.11.v_in), custom_call_target="tpu_custom_call" | custom-call | tf_op jit(solution)/shard_map/finish/pallas_call | solution.py:320
